TPU v7x, 32 devices: a whole 2x2x4 slice. The times are simulated.
32 devices in a mesh: group: 2 (over y), section: 4 (over x, core), tensor: 4 (over z).
Axes of the slice: x: 2, y: 2, z: 4, core: 2. Of those that a mesh axis runs over, the one named last changes fastest.
Arguments:
- hidden_states: bfloat16 [2, 4, 4, 8192], P('group', 'section', 'tensor'), may hold values from -6 to 6
- query_train: bfloat16 [4, 8192, 4096], P(None, ('group', 'section'), 'tensor'), may hold values from -0.0625 to 0.0625
- keyval_train: bfloat16 [4, 8192, 1024], P(None, ('group', 'section'), 'tensor'), may hold values from -0.0625 to 0.0625
- layer_of_section: int32 [4], replicated, may hold values from 0 to 3, each once
- lengths: int32 [2, 4, 4], P('group', 'section', 'tensor'), may hold values from 2 to 1024
- kv_cache: bfloat16 [2, 4, 4, 1024, 1024], P('group', 'section', 'tensor'), as said below
Outputs:
- attended: bfloat16 [2, 4, 4, 4096], P('group', 'section', 'tensor')
- new_entries: bfloat16 [2, 4, 4, 1024], P('group', 'section', 'tensor')
Inputs may be any that keep to these rules, and one draw needn't show every extreme that they name: `layer_of_section`: every layer appears once. `kv_cache`: cache positions at or past a sequence's length hold entries that are never read.
All inputs are finite; a program needn't handle non-finite values.
Results may differ from a plain program's by a relative error of at most 0.03.
Values may be sent and summed in bfloat16 or wider, within the bound.
A program may use at most 64 MiB of HBM per device.

v0:
```python
import jax
import jax.numpy as jnp
from jax import lax
from jax.sharding import PartitionSpec as P

HD = 128
QH = 32
KVH = 4


def rotate(vectors, position):
    half_size = HD // 2
    inverse = jnp.power(jnp.float32(500000.0), -jnp.arange(half_size, dtype=jnp.float32) * 2.0 / HD)
    angle = position[:, None, None] * inverse[None, None, :]
    cosine = jnp.cos(angle)
    sine_part = jnp.sin(angle)
    first_half = vectors[..., :half_size]
    second = vectors[..., half_size:]
    return jnp.concatenate(
        [first_half * cosine - second * sine_part, second * cosine + first_half * sine_part],
        axis=-1,
    )


def attend(queries, key_value, seq_lens, cache):
    count = queries.shape[0]
    cache_len = cache.shape[1]
    per_kv = QH // KVH
    position = seq_lens.astype(jnp.float32)
    query_rot = rotate(queries.astype(jnp.float32).reshape(count, QH, HD), position).astype(
        jnp.bfloat16
    )
    key_rot = rotate(
        key_value[:, : KVH * HD].astype(jnp.float32).reshape(count, KVH, HD), position
    ).astype(jnp.bfloat16)
    new_values = key_value[:, KVH * HD :]
    cache_keys = cache[:, :, : KVH * HD].reshape(count, cache_len, KVH, HD)
    cache_values = cache[:, :, KVH * HD :].reshape(count, cache_len, KVH, HD)
    query_group = query_rot.reshape(count, KVH, per_kv, HD)
    score_scale = 1.0 / jnp.sqrt(jnp.float32(HD))
    scores = (
        jnp.einsum("skgd,sjkd->skgj", query_group, cache_keys, preferred_element_type=jnp.float32)
        * score_scale
    )
    own_score = (
        jnp.einsum("skgd,skd->skg", query_group, key_rot, preferred_element_type=jnp.float32)
        * score_scale
    )
    usable = (jnp.arange(cache_len, dtype=jnp.int32)[None, :] < seq_lens[:, None])[:, None, None, :]
    scores = jnp.where(usable, scores, jnp.float32(-1e30))
    largest = jnp.maximum(jnp.max(scores, axis=-1), own_score)
    exponent = jnp.where(usable, jnp.exp(scores - largest[..., None]), jnp.float32(0.0))
    own_exp = jnp.exp(own_score - largest)
    totals = jnp.sum(exponent, axis=-1) + own_exp
    probs = (exponent / totals[..., None]).astype(jnp.bfloat16)
    own_prob = (own_exp / totals).astype(jnp.bfloat16)
    new_float = new_values.astype(jnp.float32).reshape(count, KVH, HD)
    result = jnp.einsum("skgj,sjkd->skgd", probs, cache_values, preferred_element_type=jnp.float32)
    result = result + own_prob.astype(jnp.float32)[..., None] * new_float[:, :, None, :]
    entries = jnp.concatenate([key_rot.reshape(count, KVH * HD), new_values], axis=1)
    return (result.reshape(count, QH * HD).astype(jnp.bfloat16), entries)


def shards(hidden_states, query_train, keyval_train, layer_of_section, lengths, kv_cache):
    all_tokens = lax.all_gather(hidden_states[0, 0], "tensor", axis=0, tiled=True)
    query_sorted = query_train[layer_of_section]
    keyval_sorted = keyval_train[layer_of_section]
    moved = (
        lax.all_to_all(query_sorted, "section", split_axis=0, concat_axis=1, tiled=True),
        lax.all_to_all(keyval_sorted, "section", split_axis=0, concat_axis=1, tiled=True),
    )
    query_cols = moved[0].shape[2]
    batch_rows = all_tokens.shape[0]
    group_count = lax.axis_size("group")
    row_count = moved[0].shape[1]
    blocks = all_tokens.reshape(1, batch_rows, group_count, row_count)
    arrived = lax.all_to_all(blocks, "group", split_axis=2, concat_axis=0, tiled=True)
    w_both = jnp.concatenate([moved[0][0], moved[1][0]], axis=1)
    both_parts = lax.psum_scatter(
        jnp.einsum("gbr,rc->gbc", arrived[:, :, 0, :], w_both, preferred_element_type=jnp.float32),
        "group",
        scatter_dimension=0,
        tiled=True,
    )[0]
    query_part = both_parts[:, :query_cols]
    keyval_part = both_parts[:, query_cols:]
    queries = query_part.astype(jnp.bfloat16)
    key_value = keyval_part.astype(jnp.bfloat16)
    query_seq, keyval_seq = (
        lax.all_to_all(queries, "tensor", split_axis=0, concat_axis=1, tiled=True),
        lax.all_to_all(key_value, "tensor", split_axis=0, concat_axis=1, tiled=True),
    )
    result, entries = attend(query_seq, keyval_seq, lengths[0, 0], kv_cache[0, 0])
    return (result[None, None], entries[None, None])


def solution(mesh):
    in_specs = (
        P("group", "section", "tensor", None),
        P(None, ("group", "section"), "tensor"),
        P(None, ("group", "section"), "tensor"),
        P(),
        P("group", "section", "tensor"),
        P("group", "section", "tensor", None, None),
    )
    out_specs = (P("group", "section", "tensor", None), P("group", "section", "tensor", None))
    return jax.shard_map(shards, mesh=mesh, in_specs=in_specs, out_specs=out_specs, check_vma=False)
```

profile of v0, /device:TPU:0, one launch (start us, length us, event | category | flops | bytes accessed | tf_op | source)
XLA Modules:
  0.0 190.8 jit_solution(7543319990391198501)
XLA Ops:
  0.6 15.4 %all-gather = bf16[4,1,1,8192]{3,2,1,0:T(2,128)(2,1)S(1)} all-gather(bf16[1,1,1,8192]{3,2,1,0:T(2,128)(2,1)} %param.6), channel_id=2, replica_groups=mesh['group'=2,'section'=4,'tensor'=4] {'tensor'}, dimensions={0}, use_global_device_ids=true | all-gather | bytes 81920 | tf_op jit(solution)/shard_map/all_gather | solution.py:65
  16.1 1.0 reduce.4
  17.1 3.3 %all-to-all-start.2 = ((bf16[1,4,2,4096]{3,1,0,2:T(4,128)(2,1)}), bf16[1,4,2,4096]{3,1,0,2:T(4,128)(2,1)S(1)}, u32[]{:S(2)}, u32[]{:S(2)}) async-start(bf16[1,4,2,4096]{3,1,0,2:T(4,128)(2,1)} %bitcast.30), calls=%async_computation.2 | async-start | bytes 131072 | tf_op jit(solution)/shard_map/all_to_all | solution.py:77
  20.4 0.7 compare_select_fusion
  21.1 2.0 %gather_fusion = bf16[4,1024,256]{2,1,0:T(8,128)(2,1)} fusion(bf16[4,1024,256]{2,1,0:T(8,128)(2,1)S(1)} %copy-done, s32[1024]{0:T(1024)S(1)} %pad_clamp_fusion), kind=kCustom, calls=%fused_computation | custom fusion | bytes 4194320 | tf_op jit(solution)/shard_map/gather | solution.py:67
  23.0 1.4 all-to-all-done.2
  24.5 4.4 %all-to-all-start.1 = ((bf16[4,1024,256]{2,1,0:T(8,128)(2,1)}), bf16[4,1024,256]{2,1,0:T(8,128)(2,1)}, u32[]{:S(2)}, u32[]{:S(2)}) async-start(bf16[4,1024,256]{2,1,0:T(8,128)(2,1)} %gather_fusion), calls=%async_computation.1 | async-start | bytes 4194304 | tf_op jit(solution)/shard_map/all_to_all | solution.py:70
  28.9 5.9 %fusion.23 = (bf16[4,512,1024]{2,1,0:T(8,128)(2,1)}, bf16[4,512,1024]{2,1,0:T(8,128)(2,1)}) fusion(bf16[4,1024,1024]{2,1,0:T(8,128)(2,1)} %param.7), kind=kLoop, calls=%fused_computation.53 | loop fusion | bytes 16777216 | tf_op jit(solution)/shard_map/gather | solution.py:66
  34.8 5.0 %gather_fusion.1 = bf16[4,512,1024]{2,1,0:T(8,128)(2,1)} fusion(bf16[4,512,1024]{2,1,0:T(8,128)(2,1)} %get-tuple-element.2, s32[1024]{0:T(1024)S(1)} %pad_clamp_fusion), kind=kCustom, calls=%fused_computation.1 | custom fusion | bytes 8388624 | tf_op jit(solution)/shard_map/gather | solution.py:66
  39.8 4.9 %gather_fusion.2 = bf16[4,512,1024]{2,1,0:T(8,128)(2,1)} fusion(bf16[4,512,1024]{2,1,0:T(8,128)(2,1)} %get-tuple-element.3, s32[1024]{0:T(1024)S(1)} %pad_clamp_fusion), kind=kCustom, calls=%fused_computation.2 | custom fusion | bytes 8388624 | tf_op jit(solution)/shard_map/gather | solution.py:66
  44.7 7.7 %pad_maximum_fusion = bf16[4,1024,1024]{2,1,0:T(8,128)(2,1)} fusion(bf16[4,512,1024]{2,1,0:T(8,128)(2,1)} %gather_fusion.2, bf16[4,512,1024]{2,1,0:T(8,128)(2,1)} %gather_fusion.1), kind=kLoop, calls=%fused_computation.5 | loop fusion | flops 16777216 | bytes 16777216
  52.4 2.3 %all-to-all-done.1 = bf16[4,1024,256]{2,1,0:T(8,128)(2,1)} async-done(((bf16[4,1024,256]{2,1,0:T(8,128)(2,1)}), bf16[4,1024,256]{2,1,0:T(8,128)(2,1)}, u32[]{:S(2)}, u32[]{:S(2)}) %all-to-all-start.1) | async-done | bytes 2097184 | tf_op jit(solution)/shard_map/all_to_all | solution.py:70
  54.7 5.7 %all-to-all-start = ((bf16[4,1024,1024]{2,1,0:T(8,128)(2,1)}), bf16[4,1024,1024]{2,1,0:T(8,128)(2,1)}, u32[]{:S(2)}, u32[]{:S(2)}) async-start(bf16[4,1024,1024]{2,1,0:T(8,128)(2,1)} %pad_maximum_fusion), calls=%async_computation | async-start | bytes 16777216 | tf_op jit(solution)/shard_map/all_to_all | solution.py:69
  61.0 3.9 %copy.14 = bf16[1,1,1,1024,1024]{3,4,2,1,0:T(8,128)(2,1)} copy(bf16[1,1,1,1024,1024]{4,3,2,1,0:T(8,128)(2,1)} %param.11) | data formatting | bytes 4194304 | tf_op args[5]
  65.6 2.7 %fusion.24 = (bf16[1,1024,512]{1,2,0:T(8,128)(2,1)}, bf16[1,1024,512]{1,2,0:T(8,128)(2,1)S(1)}) fusion(bf16[1,1024,1024]{1,2,0:T(8,128)(2,1)} %bitcast.53), kind=kLoop, calls=%fused_computation.54 | loop fusion | bytes 4194304 | tf_op jit(solution)/shard_map/slice | solution.py:37
  68.3 85.2 %all-to-all-done = bf16[4,1024,1024]{2,1,0:T(8,128)(2,1)} async-done(((bf16[4,1024,1024]{2,1,0:T(8,128)(2,1)}), bf16[4,1024,1024]{2,1,0:T(8,128)(2,1)}, u32[]{:S(2)}, u32[]{:S(2)}) %all-to-all-start) | async-done | bytes 8388640 | tf_op jit(solution)/shard_map/all_to_all | solution.py:69
  153.5 4.9 %fusion.1 = f32[2,4,1280]{2,1,0:T(4,128)S(1)} fusion(bf16[4096,256]{1,0:T(8,128)(2,1)} %bitcast.2, bf16[4096,1024]{1,0:T(8,128)(2,1)} %bitcast.1, bf16[1,4,2,4096]{3,1,0,2:T(4,128)(2,1)S(1)} %all-to-all-done.2), kind=kOutput, calls=%fused_computation.6 | convolution fusion | flops 104857600 | bytes 10592256 | tf_op jit(solution)/shard_map/gbr,rc->gbc/dot_general | solution.py:80
  158.4 7.6 %all-reduce = bf16[2,4,1280]{2,1,0:T(4,128)(2,1)S(1)} all-reduce(f32[2,4,1280]{2,1,0:T(4,128)S(1)} %fusion.1), channel_id=3, replica_groups=mesh['group'=2,'section'=4,'tensor'=4] {'group'}, use_global_device_ids=true, to_apply=%region_0.0.clone | all-reduce | flops 10240 | bytes 61440
  168.4 5.0 %all-to-all-start.4 = ((bf16[4,2,128]{2,1,0:T(2,128)(2,1)}), bf16[4,2,128]{2,1,0:T(2,128)(2,1)S(1)}, u32[]{:S(2)}, u32[]{:S(2)}) async-start(bf16[4,2,128]{2,1,0:T(2,128)(2,1)} %reshape.255), calls=%async_computation.4 | async-start | bytes 4096 | tf_op jit(solution)/shard_map/all_to_all | solution.py:91
  173.3 0.7 reduce.5
  174.6 4.2 %all-to-all-done.4 = bf16[4,2,128]{2,1,0:T(2,128)(2,1)S(1)} async-done(((bf16[4,2,128]{2,1,0:T(2,128)(2,1)}), bf16[4,2,128]{2,1,0:T(2,128)(2,1)S(1)}, u32[]{:S(2)}, u32[]{:S(2)}) %all-to-all-start.4) | async-done | bytes 2080 | tf_op jit(solution)/shard_map/all_to_all | solution.py:91
  178.8 3.2 %all-to-all-start.3 = ((bf16[4,2,512]{2,1,0:T(2,128)(2,1)}), bf16[4,2,512]{2,1,0:T(2,128)(2,1)S(1)}, u32[]{:S(2)}, u32[]{:S(2)}) async-start(bf16[4,2,512]{2,1,0:T(2,128)(2,1)} %reshape.253), calls=%async_computation.3 | async-start | bytes 16384 | tf_op jit(solution)/shard_map/all_to_all | solution.py:90
  183.0 4.7 %all-to-all-done.3 = bf16[4,2,512]{2,1,0:T(2,128)(2,1)S(1)} async-done(((bf16[4,2,512]{2,1,0:T(2,128)(2,1)}), bf16[4,2,512]{2,1,0:T(2,128)(2,1)S(1)}, u32[]{:S(2)}, u32[]{:S(2)}) %all-to-all-start.3) | async-done | bytes 8224 | tf_op jit(solution)/shard_map/all_to_all | solution.py:90
  188.0 1.6 fusion.26
  (31 shorter events, 6.1 us)
Async XLA Ops:
  0.6 20.4 %copy-start = (bf16[4,1024,256]{2,1,0:T(8,128)(2,1)S(1)}, bf16[4,1024,256]{2,1,0:T(8,128)(2,1)}, u32[]{:S(2)}) copy-start(bf16[4,1024,256]{2,1,0:T(8,128)(2,1)} %param.8) | copy-start | bytes 6291460
  17.1 7.4 %all-to-all-start.2 = ((bf16[1,4,2,4096]{3,1,0,2:T(4,128)(2,1)}), bf16[1,4,2,4096]{3,1,0,2:T(4,128)(2,1)S(1)}, u32[]{:S(2)}, u32[]{:S(2)}) async-start(bf16[1,4,2,4096]{3,1,0,2:T(4,128)(2,1)} %bitcast.30), calls=%async_computation.2 | async-start | bytes 131072 | tf_op jit(solution)/shard_map/all_to_all | solution.py:77
  24.5 30.2 %all-to-all-start.1 = ((bf16[4,1024,256]{2,1,0:T(8,128)(2,1)}), bf16[4,1024,256]{2,1,0:T(8,128)(2,1)}, u32[]{:S(2)}, u32[]{:S(2)}) async-start(bf16[4,1024,256]{2,1,0:T(8,128)(2,1)} %gather_fusion), calls=%async_computation.1 | async-start | bytes 4194304 | tf_op jit(solution)/shard_map/all_to_all | solution.py:70
  54.7 98.8 %all-to-all-start = ((bf16[4,1024,1024]{2,1,0:T(8,128)(2,1)}), bf16[4,1024,1024]{2,1,0:T(8,128)(2,1)}, u32[]{:S(2)}, u32[]{:S(2)}) async-start(bf16[4,1024,1024]{2,1,0:T(8,128)(2,1)} %pad_maximum_fusion), calls=%async_computation | async-start | bytes 16777216 | tf_op jit(solution)/shard_map/all_to_all | solution.py:69
  60.4 4.6 %copy-start.1 = (u32[32]{0:T(128)S(1)}, u32[32]{0:T(128)}, u32[]{:S(2)}) copy-start(u32[32]{0:T(128)} %constant.26) | copy-start | bytes 388
  168.4 10.5 %all-to-all-start.4 = ((bf16[4,2,128]{2,1,0:T(2,128)(2,1)}), bf16[4,2,128]{2,1,0:T(2,128)(2,1)S(1)}, u32[]{:S(2)}, u32[]{:S(2)}) async-start(bf16[4,2,128]{2,1,0:T(2,128)(2,1)} %reshape.255), calls=%async_computation.4 | async-start | bytes 4096 | tf_op jit(solution)/shard_map/all_to_all | solution.py:91
  178.8 8.8 %all-to-all-start.3 = ((bf16[4,2,512]{2,1,0:T(2,128)(2,1)}), bf16[4,2,512]{2,1,0:T(2,128)(2,1)S(1)}, u32[]{:S(2)}, u32[]{:S(2)}) async-start(bf16[4,2,512]{2,1,0:T(2,128)(2,1)} %reshape.253), calls=%async_computation.3 | async-start | bytes 16384 | tf_op jit(solution)/shard_map/all_to_all | solution.py:90
where the time goes:
time: 192 us; the launch traced here: 191 us
  waiting for transfers between devices  97.8 us (51%)
  local copies, waits for them, and re-layouts  28.1 us (15%)
  blocking collectives  23 us (12%)
  starting transfers between devices  21.6 us (11%)
  other arithmetic  11.8 us (6%)
  matrix products  7.11 us (4%)
    all_to_all x1, waiting for transfers between devices, shards(): lax.all_to_all(query_sorted, 'section', split_axis=0, concat_axis=1, tile...  85.2 us
    gather x3, local copies, waits for them, and re-layouts, shards(): query_sorted = query_train[layer_of_section]  15.8 us
    all_gather x1, blocking collectives, shards(): lax.all_gather(hidden_states[0, 0], 'tensor', axis=0, tiled=True)  15.4 us
    unnamed x2, other arithmetic  7.75 us
    unnamed x1, blocking collectives  7.55 us
    unnamed x11, local copies, waits for them, and re-layouts  5.77 us
    all_to_all x1, starting transfers between devices, shards(): lax.all_to_all(query_sorted, 'section', split_axis=0, concat_axis=1, tile...  5.67 us
    all_to_all x1, starting transfers between devices, shards(): lax.all_to_all(key_value, 'tensor', split_axis=0, concat_axis=1, tiled=True)  4.97 us
  transfers between devices with their start and end apart: 5, of which 5 were waited for; matrix products, arithmetic and copies ran while one was open for 19% of the time, Pallas kernels for 0%

commit v1 on v0

--- a/solution.py
+++ b/solution.py
@@ -6,6 +6,14 @@
 HD = 128
 QH = 32
 KVH = 4
+
+
+def _choose_axis_part(page, chip_axis):
+    r2 = lax.axis_size(chip_axis)
+    local_next = jnp.split(page, r2, axis=0)
+    carry_in = jnp.stack(local_next)
+    t_next = lax.all_to_all(carry_in, chip_axis, 0, 0)
+    return jnp.concatenate(t_next, 1)
 
 
 def rotate(vectors, position):
@@ -66,7 +74,7 @@
     query_sorted = query_train[layer_of_section]
     keyval_sorted = keyval_train[layer_of_section]
     moved = (
-        lax.all_to_all(query_sorted, "section", split_axis=0, concat_axis=1, tiled=True),
+        _choose_axis_part(query_sorted, "section"),
         lax.all_to_all(keyval_sorted, "section", split_axis=0, concat_axis=1, tiled=True),
     )
     query_cols = moved[0].shape[2]

time: 192 us -> 217 us (1.13)
  waiting for transfers between devices: 97.8 us -> 115 us
  local copies, waits for them, and re-layouts: 28.1 us -> 38.5 us
  other arithmetic: 11.8 us -> 8.02 us
    all_to_all x1, waiting for transfers between devices: 2.26 us -> 18 us  [shards(): lax.all_to_all(keyval_sorted, 'section', split_axis=0, concat_axis=1, til...]
    unnamed x11 -> x15, local copies, waits for them, and re-layouts: 5.77 us -> 13.9 us
    unnamed x2 -> x1, other arithmetic: 7.75 us -> 0.08 us
    another operation x1 -> x2, local copies, waits for them, and re-layouts: 0.66 us -> 4.53 us  [the longest x1 3.88 us: _choose_axis_part(): carry_in = jnp.stack(local_next)]
    another operation x1 -> x2, other arithmetic: 0.08 us -> 3.9 us  [the longest x1 3.83 us: _choose_axis_part(): carry_in = jnp.stack(local_next)]
    all_to_all x1, waiting for transfers between devices: 85.2 us -> 87.8 us  [_choose_axis_part(): t_next = lax.all_to_all(carry_in, chip_axis, 0, 0)]
  transfers between devices with their start and end apart: 5 -> 5, of which waited for: 5 -> 4; matrix products, arithmetic and copies ran while one was open for 19% -> 20% of each run, Pallas kernels for 0% -> 0%
where the time goes in v1:
time: 217 us; the launch traced here: 216 us
  waiting for transfers between devices  115 us (53%)
  local copies, waits for them, and re-layouts  38.5 us (18%)
  blocking collectives  24.4 us (11%)
  starting transfers between devices  21.6 us (10%)
  other arithmetic  8.02 us (4%)
  matrix products  7.24 us (3%)
    all_to_all x1, waiting for transfers between devices, _choose_axis_part(): t_next = lax.all_to_all(carry_in, chip_axis, 0, 0)  87.8 us
    all_to_all x1, waiting for transfers between devices, shards(): lax.all_to_all(keyval_sorted, 'section', split_axis=0, concat_axis=1, til...  18 us
    gather x3, local copies, waits for them, and re-layouts, shards(): query_sorted = query_train[layer_of_section]  15.8 us
    all_gather x1, blocking collectives, shards(): lax.all_gather(hidden_states[0, 0], 'tensor', axis=0, tiled=True)  15.4 us
    unnamed x15, local copies, waits for them, and re-layouts  13.9 us
    unnamed x1, blocking collectives  9 us
    all_to_all x1, starting transfers between devices, _choose_axis_part(): t_next = lax.all_to_all(carry_in, chip_axis, 0, 0)  5.63 us
    dot_general x1, matrix products, shards(): jnp.einsum('gbr,rc->gbc', arrived[:, :, 0, :], w_both, preferred_element_...  5 us
  transfers between devices with their start and end apart: 5, of which 4 were waited for; matrix products, arithmetic and copies ran while one was open for 20% of the time, Pallas kernels for 0%

profile of v1, /device:TPU:0, one launch (start us, length us, event | category | flops | bytes accessed | tf_op | source)
XLA Modules:
  0.0 215.9 jit_solution(14754524049636812660)
XLA Ops:
  0.6 15.4 %all-gather = bf16[4,1,1,8192]{3,2,1,0:T(2,128)(2,1)S(1)} all-gather(bf16[1,1,1,8192]{3,2,1,0:T(2,128)(2,1)} %param.6), channel_id=2, replica_groups=mesh['group'=2,'section'=4,'tensor'=4] {'tensor'}, dimensions={0}, use_global_device_ids=true | all-gather | bytes 81920 | tf_op jit(solution)/shard_map/all_gather | solution.py:73
  16.1 1.0 reduce.4
  17.1 3.3 %all-to-all-start.2 = ((bf16[1,4,2,4096]{3,1,0,2:T(4,128)(2,1)}), bf16[1,4,2,4096]{3,1,0,2:T(4,128)(2,1)S(1)}, u32[]{:S(2)}, u32[]{:S(2)}) async-start(bf16[1,4,2,4096]{3,1,0,2:T(4,128)(2,1)} %bitcast.34), calls=%async_computation.2 | async-start | bytes 131072 | tf_op jit(solution)/shard_map/all_to_all | solution.py:85
  21.1 5.9 %fusion.23 = (bf16[4,512,1024]{2,1,0:T(8,128)(2,1)}, bf16[4,512,1024]{2,1,0:T(8,128)(2,1)}) fusion(bf16[4,1024,1024]{2,1,0:T(8,128)(2,1)} %param.7), kind=kLoop, calls=%fused_computation.59 | loop fusion | bytes 16777216 | tf_op jit(solution)/shard_map/gather | solution.py:74
  27.0 4.9 %gather_fusion.1 = bf16[4,512,1024]{2,1,0:T(8,128)(2,1)} fusion(bf16[4,512,1024]{2,1,0:T(8,128)(2,1)} %get-tuple-element.7, s32[1024]{0:T(1024)S(1)} %pad_clamp_fusion), kind=kCustom, calls=%fused_computation.1 | custom fusion | bytes 8388624 | tf_op jit(solution)/shard_map/gather | solution.py:74
  31.9 4.6 %constant_dynamic-update-slice_fusion.1 = bf16[4,1024,1024]{2,1,0:T(8,128)(2,1)} fusion(bf16[4,512,1024]{2,1,0:T(8,128)(2,1)} %gather_fusion.1), kind=kLoop, calls=%fused_computation.33 | loop fusion | bytes 8388608
  36.5 4.9 %gather_fusion.2 = bf16[4,512,1024]{2,1,0:T(8,128)(2,1)} fusion(bf16[4,512,1024]{2,1,0:T(8,128)(2,1)} %get-tuple-element.6, s32[1024]{0:T(1024)S(1)} %pad_clamp_fusion), kind=kCustom, calls=%fused_computation.2 | custom fusion | bytes 8388624 | tf_op jit(solution)/shard_map/gather | solution.py:74
  41.5 4.6 %constant_dynamic-update-slice_fusion = bf16[4,1024,1024]{2,1,0:T(8,128)(2,1)} fusion(bf16[4,1024,1024]{2,1,0:T(8,128)(2,1)} %constant_dynamic-update-slice_fusion.1, bf16[4,512,1024]{2,1,0:T(8,128)(2,1)} %gather_fusion.2), kind=kLoop, calls=%fused_computation.32 | loop fusion | bytes 8388608
  46.1 2.0 gather_fusion
  48.0 4.4 %all-to-all-start.1 = ((bf16[4,1024,256]{2,1,0:T(8,128)(2,1)}), bf16[4,1024,256]{2,1,0:T(8,128)(2,1)}, u32[]{:S(2)}, u32[]{:S(2)}) async-start(bf16[4,1024,256]{2,1,0:T(8,128)(2,1)} %gather_fusion), calls=%async_computation.1 | async-start | bytes 4194304 | tf_op jit(solution)/shard_map/all_to_all | solution.py:78
  52.5 3.9 %slice_bitcast_fusion.3 = (bf16[1,1,1024,1024]{3,2,1,0:T(8,128)(2,1)S(1)}, bf16[1,1,1024,1024]{3,2,1,0:T(8,128)(2,1)S(1)}, bf16[1,1,1024,1024]{3,2,1,0:T(8,128)(2,1)S(1)}, bf16[1,1,1024,1024]{3,2,1,0:T(8,128)(2,1)S(1)}) fusion(bf16[4,1024,1024]{2,1,0:T(8,128)(2,1)} %constant_dynamic-update-slice_fusion), kind=kLoop, calls=%fused_computation.10 | loop fusion | bytes 16777216 | tf_op jit(solution)/shard_map/stack | solution.py:14
  56.4 3.8 %pad_maximum_fusion = bf16[4,1,1024,1024]{3,2,1,0:T(8,128)(2,1)} fusion(bf16[1,1,1024,1024]{3,2,1,0:T(8,128)(2,1)S(1)} %get-tuple-element.3, bf16[1,1,1024,1024]{3,2,1,0:T(8,128)(2,1)S(1)} %get-tuple-element.4, bf16[1,1,1024,1024]{3,2,1,0:T(8,128)(2,1)S(1)} %get-tuple-element.5, bf16[1,1,1024,1024]{3,2,1,0:T(8,128)(2,1)S(1)} %get-tuple-element.2), kind=kLoop, calls=%fused_computation.5 | loop fusion | flops 12582912 | bytes 16777216 | tf_op jit(solution)/shard_map/stack | solution.py:14
  60.2 18.0 %all-to-all-done.1 = bf16[4,1024,256]{2,1,0:T(8,128)(2,1)} async-done(((bf16[4,1024,256]{2,1,0:T(8,128)(2,1)}), bf16[4,1024,256]{2,1,0:T(8,128)(2,1)}, u32[]{:S(2)}, u32[]{:S(2)}) %all-to-all-start.1) | async-done | bytes 2097184 | tf_op jit(solution)/shard_map/all_to_all | solution.py:78
  78.2 5.6 %all-to-all-start = ((bf16[4,1,1024,1024]{3,2,1,0:T(8,128)(2,1)}), bf16[4,1,1024,1024]{3,2,1,0:T(8,128)(2,1)}, u32[]{:S(2)}, u32[]{:S(2)}) async-start(bf16[4,1,1024,1024]{3,2,1,0:T(8,128)(2,1)} %pad_maximum_fusion), calls=%async_computation | async-start | bytes 16777216 | tf_op jit(solution)/shard_map/all_to_all | solution.py:15
  84.5 2.9 %copy.14 = bf16[1,1,1,1024,1024]{3,4,2,1,0:T(8,128)(2,1)S(1)} copy(bf16[1,1,1,1024,1024]{4,3,2,1,0:T(8,128)(2,1)} %param.11) | data formatting | bytes 4194304 | tf_op args[5]
  88.1 1.2 fusion.24
  89.2 87.8 %all-to-all-done = bf16[4,1,1024,1024]{3,2,1,0:T(8,128)(2,1)} async-done(((bf16[4,1,1024,1024]{3,2,1,0:T(8,128)(2,1)}), bf16[4,1,1024,1024]{3,2,1,0:T(8,128)(2,1)}, u32[]{:S(2)}, u32[]{:S(2)}) %all-to-all-start) | async-done | bytes 8388640 | tf_op jit(solution)/shard_map/all_to_all | solution.py:15
  177.0 5.0 %fusion.1 = f32[2,4,1280]{2,1,0:T(4,128)S(1)} fusion(bf16[4096,256]{1,0:T(8,128)(2,1)} %bitcast.6, bf16[4096,1024]{1,0:T(8,128)(2,1)} %bitcast.5, bf16[1,4,2,4096]{3,1,0,2:T(4,128)(2,1)S(1)} %all-to-all-done.2), kind=kOutput, calls=%fused_computation.6 | convolution fusion | flops 104857600 | bytes 10592256 | tf_op jit(solution)/shard_map/gbr,rc->gbc/dot_general | solution.py:88
  182.0 9.0 %all-reduce = bf16[2,4,1280]{2,1,0:T(4,128)(2,1)S(1)} all-reduce(f32[2,4,1280]{2,1,0:T(4,128)S(1)} %fusion.1), channel_id=3, replica_groups=mesh['group'=2,'section'=4,'tensor'=4] {'group'}, use_global_device_ids=true, to_apply=%region_0.0.clone | all-reduce | flops 10240 | bytes 61440
  193.5 5.0 %all-to-all-start.4 = ((bf16[4,2,128]{2,1,0:T(2,128)(2,1)}), bf16[4,2,128]{2,1,0:T(2,128)(2,1)S(1)}, u32[]{:S(2)}, u32[]{:S(2)}) async-start(bf16[4,2,128]{2,1,0:T(2,128)(2,1)} %reshape.251), calls=%async_computation.4 | async-start | bytes 4096 | tf_op jit(solution)/shard_map/all_to_all | solution.py:99
  199.7 4.2 %all-to-all-done.4 = bf16[4,2,128]{2,1,0:T(2,128)(2,1)S(1)} async-done(((bf16[4,2,128]{2,1,0:T(2,128)(2,1)}), bf16[4,2,128]{2,1,0:T(2,128)(2,1)S(1)}, u32[]{:S(2)}, u32[]{:S(2)}) %all-to-all-start.4) | async-done | bytes 2080 | tf_op jit(solution)/shard_map/all_to_all | solution.py:99
  203.9 3.2 %all-to-all-start.3 = ((bf16[4,2,512]{2,1,0:T(2,128)(2,1)}), bf16[4,2,512]{2,1,0:T(2,128)(2,1)S(1)}, u32[]{:S(2)}, u32[]{:S(2)}) async-start(bf16[4,2,512]{2,1,0:T(2,128)(2,1)} %reshape.249), calls=%async_computation.3 | async-start | bytes 16384 | tf_op jit(solution)/shard_map/all_to_all | solution.py:98
  208.0 4.7 %all-to-all-done.3 = bf16[4,2,512]{2,1,0:T(2,128)(2,1)S(1)} async-done(((bf16[4,2,512]{2,1,0:T(2,128)(2,1)}), bf16[4,2,512]{2,1,0:T(2,128)(2,1)S(1)}, u32[]{:S(2)}, u32[]{:S(2)}) %all-to-all-start.3) | async-done | bytes 8224 | tf_op jit(solution)/shard_map/all_to_all | solution.py:98
  213.0 1.6 fusion.26
  (36 shorter events, 7.5 us)
Async XLA Ops:
  0.6 45.4 %copy-start = (bf16[4,1024,256]{2,1,0:T(8,128)(2,1)S(1)}, bf16[4,1024,256]{2,1,0:T(8,128)(2,1)}, u32[]{:S(2)}) copy-start(bf16[4,1024,256]{2,1,0:T(8,128)(2,1)} %param.8) | copy-start | bytes 6291460
  17.1 30.9 %all-to-all-start.2 = ((bf16[1,4,2,4096]{3,1,0,2:T(4,128)(2,1)}), bf16[1,4,2,4096]{3,1,0,2:T(4,128)(2,1)S(1)}, u32[]{:S(2)}, u32[]{:S(2)}) async-start(bf16[1,4,2,4096]{3,1,0,2:T(4,128)(2,1)} %bitcast.34), calls=%async_computation.2 | async-start | bytes 131072 | tf_op jit(solution)/shard_map/all_to_all | solution.py:85
  48.0 30.2 %all-to-all-start.1 = ((bf16[4,1024,256]{2,1,0:T(8,128)(2,1)}), bf16[4,1024,256]{2,1,0:T(8,128)(2,1)}, u32[]{:S(2)}, u32[]{:S(2)}) async-start(bf16[4,1024,256]{2,1,0:T(8,128)(2,1)} %gather_fusion), calls=%async_computation.1 | async-start | bytes 4194304 | tf_op jit(solution)/shard_map/all_to_all | solution.py:78
  78.2 98.8 %all-to-all-start = ((bf16[4,1,1024,1024]{3,2,1,0:T(8,128)(2,1)}), bf16[4,1,1024,1024]{3,2,1,0:T(8,128)(2,1)}, u32[]{:S(2)}, u32[]{:S(2)}) async-start(bf16[4,1,1024,1024]{3,2,1,0:T(8,128)(2,1)} %pad_maximum_fusion), calls=%async_computation | async-start | bytes 16777216 | tf_op jit(solution)/shard_map/all_to_all | solution.py:15
  83.9 3.6 %copy-start.2 = (u32[32]{0:T(128)S(1)}, u32[32]{0:T(128)}, u32[]{:S(2)}) copy-start(u32[32]{0:T(128)} %constant.26) | copy-start | bytes 388
  177.0 38.9 %copy-start.1 = (bf16[4,1024,256]{2,1,0:T(8,128)(2,1)S(1)}, bf16[4,1024,256]{2,1,0:T(8,128)(2,1)}, u32[]{:S(2)}) copy-start(bf16[4,1024,256]{2,1,0:T(8,128)(2,1)} %param.8) | copy-start | bytes 6291460
  193.5 10.5 %all-to-all-start.4 = ((bf16[4,2,128]{2,1,0:T(2,128)(2,1)}), bf16[4,2,128]{2,1,0:T(2,128)(2,1)S(1)}, u32[]{:S(2)}, u32[]{:S(2)}) async-start(bf16[4,2,128]{2,1,0:T(2,128)(2,1)} %reshape.251), calls=%async_computation.4 | async-start | bytes 4096 | tf_op jit(solution)/shard_map/all_to_all | solution.py:99
  203.9 8.8 %all-to-all-start.3 = ((bf16[4,2,512]{2,1,0:T(2,128)(2,1)}), bf16[4,2,512]{2,1,0:T(2,128)(2,1)S(1)}, u32[]{:S(2)}, u32[]{:S(2)}) async-start(bf16[4,2,512]{2,1,0:T(2,128)(2,1)} %reshape.249), calls=%async_computation.3 | async-start | bytes 16384 | tf_op jit(solution)/shard_map/all_to_all | solution.py:98
